TPU v7x, 256 devices: a whole 4x4x8 slice. The times are simulated.
256 devices in a mesh: dp: 16 (over x, z_hi, core), expert: 16 (over y, z_lo).
Axes of the slice: x: 4, y: 4, z: 8 (z_hi: 2, z_lo: 4; z = z_hi * 4 + z_lo), core: 2. Of those that a mesh axis runs over, the one named last changes fastest.
Arguments:
- hidden: bfloat16 [16, 2048, 1792], P('expert', 'dp'), may hold values from -6 to 6
- outgrad: bfloat16 [16, 2048, 4096], P('expert', 'dp'), may hold values from -6 to 6
- row_expert: int32 [16, 2048], P('expert', 'dp'), may hold values from 0 to 1
- counts: int32 [16, 16], P('expert', 'dp'), may hold values from 1 to 128, as said below
- learner_map: int32 [256], replicated, may hold values from 0 to 255, as said below
- rollout_map: int32 [256], replicated, may hold values from 0 to 255, as said below
- master: float32 [4096, 28672], P('dp', 'expert'), may hold values from -3 to 3
- moment1: float32 [4096, 28672], P('dp', 'expert'), may hold values from -12 to 12
- moment2: float32 [4096, 28672], P('dp', 'expert'), may hold values from 1 to 1000
Outputs:
- new_master: float32 [4096, 28672], P('dp', 'expert')
- new_moment1: float32 [4096, 28672], P('dp', 'expert')
- new_moment2: float32 [4096, 28672], P('dp', 'expert')
- rollout_weights: bfloat16 [4096, 28672], P('dp', 'expert')
Inputs may be any that keep to these rules, and one draw needn't show every extreme that they name: `counts`: some device has exactly 128 live rows in every draw. `learner_map`: a permutation of the units. `rollout_map`: a permutation of the units; the 16 units at the positions of one learner device lie at positions of 16 different rollout devices, one each.
All inputs are finite; a program needn't handle non-finite values.
Results may differ from a plain program's by a relative error of at most 0.0095.
Values may be sent and summed in bfloat16 or wider, within the bound.
A program may use at most 128 MiB of HBM per device.

v0:
```python
import jax
import jax.numpy as jnp
from jax import lax
from jax.sharding import Mesh
from jax.sharding import PartitionSpec as P

FF = 14336
DP = ("dp_0", "dp_1", "dp_2")


beta_one = 0.9
beta_two = 0.95
learn_rate = 0.01
decay_rate = 0.1
epsilon = 1e-08
step_count = 100.0


def split_up(value, dim, devices):
    before, after = (value.shape[:dim], value.shape[dim + 1 :])
    return jnp.moveaxis(value.reshape(*before, devices, -1, *after), dim, 0)


def joined_along(blocks, dim):
    blocks = jnp.moveaxis(blocks, 0, dim)
    lengths = blocks.shape
    return blocks.reshape(*lengths[:dim], lengths[dim] * lengths[dim + 1], *lengths[dim + 2 :])


def exchange_in_order(blocks, axes, turns):
    inside = blocks.shape[1:]
    out = blocks.reshape(*(lax.axis_size(a) for a in axes), *inside)
    for k in turns:
        out = lax.all_to_all(out, axes[k], k, k, tiled=True)
    return out.reshape(-1, *inside)


def core_and_chips(value, groups, turns, split_dim, concat_dim):
    devices = lax.axis_size(groups[0]) * lax.axis_size(groups[1])
    blocks = split_up(value, split_dim, devices)
    return joined_along(exchange_in_order(blocks, groups, turns), concat_dim)


def on_device(
    hidden, outgrad, row_expert, counts, learner_map, rollout_map, master, moment1, moment2
):
    hidden = hidden[0]
    outgrad = outgrad[0]
    groups = lax.axis_size("expert")
    own_index = lax.axis_index("expert")
    block_width = hidden.shape[1] // groups
    per_expert = FF // block_width
    tok_rows = hidden.shape[0]
    width_share = master.shape[0]
    slot_units = lax.dynamic_slice_in_dim(learner_map, own_index * groups, groups)
    slot_expert = slot_units // per_expert
    live_rows = jnp.arange(tok_rows, dtype=jnp.int32) < counts[0, 0]
    kept = live_rows[:, None] & (row_expert[0][:, None] == slot_expert[None, :])
    kept_cols = jnp.repeat(kept, block_width, axis=1)
    masked = jnp.where(kept_cols, hidden, jnp.zeros((), jnp.bfloat16))
    contract = (((0,), (0,)), ((), ()))
    sliced = core_and_chips(outgrad, (("dp_0", "dp_1"), "dp_2"), (1, 0), 1, 0)
    gradient = lax.dot_general(
        sliced,
        lax.all_gather(masked, DP, axis=0, tiled=True),
        contract,
        preferred_element_type=jnp.float32,
    )
    new_moment1 = beta_one * moment1 + (1.0 - beta_one) * gradient
    new_moment2 = beta_two * moment2 + (1.0 - beta_two) * gradient * gradient
    bias_one = 1.0 - beta_one**step_count
    bias_two = 1.0 - beta_two**step_count
    update = new_moment1 / bias_one / (jnp.sqrt(new_moment2 / bias_two) + epsilon)
    new_master = master - learn_rate * (update + decay_rate * master)
    inverse_roll = jnp.argsort(rollout_map)
    inverse_learn = jnp.argsort(learner_map)
    target = inverse_roll[slot_units] // groups
    send_order = jnp.argsort(target)
    rounded = new_master.astype(jnp.bfloat16).reshape(width_share, groups, block_width)
    outgoing = jnp.take(rounded, send_order, axis=1).reshape(width_share, groups * block_width)
    incoming = lax.all_to_all(outgoing, "expert", split_axis=1, concat_axis=1, tiled=True).reshape(
        width_share, groups, block_width
    )
    wanted = lax.dynamic_slice_in_dim(rollout_map, own_index * groups, groups)
    source = inverse_learn[wanted] // groups
    rollout_weights = jnp.take(incoming, source, axis=1).reshape(width_share, groups * block_width)
    return (new_master, new_moment1, new_moment2, rollout_weights)


def solution(mesh):
    finer = Mesh(
        mesh.devices.reshape(4, 2, 2, mesh.shape["expert"]), ("dp_0", "dp_1", "dp_2", "expert")
    )
    return jax.shard_map(
        on_device,
        mesh=finer,
        in_specs=(
            P("expert", DP, None),
            P("expert", DP, None),
            P("expert", DP),
            P("expert", DP),
            P(),
            P(),
            P(DP, "expert"),
            P(DP, "expert"),
            P(DP, "expert"),
        ),
        out_specs=(P(DP, "expert"), P(DP, "expert"), P(DP, "expert"), P(DP, "expert")),
        check_vma=False,
    )
```

profile of v0, /device:TPU:1, one launch (start us, length us, event | category | flops | bytes accessed | tf_op | source)
XLA Modules:
  0.0 188.4 jit_solution(5097774377998562409)
XLA Ops:
  8.0 1.3 copy.53
  9.2 0.8 compare_select_fusion.3
  10.0 0.7 compare_and_fusion
  10.8 0.8 bitcast_select_fusion
  12.8 7.4 %all_to_all.16 = bf16[8,2,128,256]{3,2,0,1:T(8,128)(2,1)S(1)} all-to-all(bf16[8,2,128,256]{3,2,0,1:T(8,128)(2,1)S(1)} %copy.56), channel_id=1, replica_groups=mesh['dp_0'=4,'dp_1'=2,'dp_2'=2,'expert'=16] {'dp_2'}, dimensions={1} | all-to-all | bytes 2097152 | tf_op jit(solution)/shard_map/all_to_all | solution.py:34
  20.2 1.0 copy.57
  21.3 8.9 %all-to-all-start.1 = ((bf16[8,2,128,256]{3,2,1,0:T(8,128)(2,1)}), bf16[8,2,128,256]{3,2,1,0:T(8,128)(2,1)S(1)}, u32[]{:S(2)}, u32[]{:S(2)}) async-start(bf16[8,2,128,256]{3,2,1,0:T(8,128)(2,1)} %copy.57), calls=%async_computation.1 | async-start | bytes 2097152 | tf_op jit(solution)/shard_map/all_to_all | solution.py:34
  30.2 1.7 copy.52
  31.9 2.9 %copy.58 = f32[256,1792]{0,1:T(8,128)} copy(f32[256,1792]{1,0:T(8,128)} %param.19) | data formatting | bytes 3670016 | tf_op args[8]
  34.7 1.7 copy.60
  36.4 3.1 %sort.48 = (s32[256]{0:T(256)}, s32[256]{0:T(256)S(1)}) sort(s32[256]{0:T(256)S(1)} %copy-done.4, s32[256]{0:T(256)S(1)} %iota.17), dimensions={0}, to_apply=%region_0.1 | sort | flops 2048 | bytes 4096 | tf_op jit(solution)/shard_map/jit(argsort)/sort | solution.py:75
  40.2 1.2 sort.49
  41.5 19.8 %all-to-all-done.1 = bf16[8,2,128,256]{3,2,1,0:T(8,128)(2,1)S(1)} async-done(((bf16[8,2,128,256]{3,2,1,0:T(8,128)(2,1)}), bf16[8,2,128,256]{3,2,1,0:T(8,128)(2,1)S(1)}, u32[]{:S(2)}, u32[]{:S(2)}) %all-to-all-start.1) | async-done | bytes 1048608 | tf_op jit(solution)/shard_map/all_to_all | solution.py:34
  61.3 76.0 %all-gather.2.cloned.1.call-done = bf16[2048,1792]{0,1:T(8,128)(2,1)} async-done(((bf16[128,1792]{0,1:T(8,128)(2,1)}), bf16[2048,1792]{0,1:T(8,128)(2,1)}) %all-gather.2.cloned.1.call-update) | async-done | bytes 7340048 | tf_op jit(solution)/shard_map/all_gather | solution.py:65
  137.3 10.6 %fusion.1 = (bf16[256,1792]{0,1:T(8,128)(2,1)}, f32[256,1792]{0,1:T(8,128)}, f32[256,1792]{0,1:T(8,128)}, f32[256,1792]{0,1:T(8,128)S(1)}) fusion(f32[256,1792]{0,1:T(8,128)} %copy.60, f32[256,1792]{0,1:T(8,128)} %copy.52, f32[256,1792]{0,1:T(8,128)} %copy.58, bf16[2048,1792]{0,1:T(8,128)(2,1)} %all-gather.2.cloned.1.call-done, bf16[2048,256]{1,0:T(8,128)(2,1)} %bitcast.26), kind=kOutput, calls=%fused_computation.36 | convolution fusion | flops 1886388224 | bytes 20316160 | tf_op jit(solution)/shard_map/dot_general | solution.py:63
  147.9 1.8 gather_fusion.2
  149.7 1.1 select_bitcast_fusion
  150.8 4.3 %all-to-all-start.2 = ((bf16[256,16,112]{0,2,1:T(8,128)(2,1)}), bf16[256,16,112]{0,2,1:T(8,128)(2,1)S(1)}, u32[]{:S(2)}, u32[]{:S(2)}) async-start(bf16[256,16,112]{0,2,1:T(8,128)(2,1)} %select_bitcast_fusion), calls=%async_computation.2 | async-start | bytes 1835008 | tf_op jit(solution)/shard_map/all_to_all | solution.py:81
  155.1 3.2 %sort.50 = (s32[256]{0:T(256)}, s32[256]{0:T(256)S(1)}) sort(s32[256]{0:T(256)S(1)} %copy-done.5, s32[256]{0:T(256)S(1)} %iota.19), dimensions={0}, to_apply=%region_2.4 | sort | flops 2048 | bytes 4096 | tf_op jit(solution)/shard_map/jit(argsort)/sort | solution.py:76
  159.0 2.7 %copy.61 = f32[256,1792]{1,0:T(8,128)} copy(f32[256,1792]{0,1:T(8,128)} %get-tuple-element.34) | data formatting | bytes 3670016
  161.7 2.7 %copy.62 = f32[256,1792]{1,0:T(8,128)} copy(f32[256,1792]{0,1:T(8,128)} %get-tuple-element.35) | data formatting | bytes 3670016
  164.5 1.7 copy.63
  166.1 13.3 %all-to-all-done.2 = bf16[256,16,112]{0,2,1:T(8,128)(2,1)S(1)} async-done(((bf16[256,16,112]{0,2,1:T(8,128)(2,1)}), bf16[256,16,112]{0,2,1:T(8,128)(2,1)S(1)}, u32[]{:S(2)}, u32[]{:S(2)}) %all-to-all-start.2) | async-done | bytes 917536 | tf_op jit(solution)/shard_map/all_to_all | solution.py:81
  180.2 1.4 copy.64
  (32 shorter events, 3.4 us)
Async XLA Ops:
  7.2 4.4 %copy-start.2 = (bf16[1,128,4096]{2,1,0:T(8,128)(2,1)S(1)}, bf16[1,128,4096]{2,1,0:T(8,128)(2,1)}, u32[]{:S(2)}) copy-start(bf16[1,128,4096]{2,1,0:T(8,128)(2,1)} %param.12) | copy-start | bytes 3145732
  7.2 130.2 %all-gather.2.cloned.1.call-start = ((), (), s32[]{:S(2)}) async-start(), calls=%async_computation.3 | async-start | bytes 7798784 | tf_op jit(solution)/shard_map/all_gather | solution.py:65
  20.2 10.0 %copy-start = (f32[256,1792]{1,0:T(8,128)S(1)}, f32[256,1792]{1,0:T(8,128)}, u32[]{:S(2)}) copy-start(f32[256,1792]{1,0:T(8,128)} %param.18) | copy-start | bytes 5505028
  21.3 40.1 %all-to-all-start.1 = ((bf16[8,2,128,256]{3,2,1,0:T(8,128)(2,1)}), bf16[8,2,128,256]{3,2,1,0:T(8,128)(2,1)S(1)}, u32[]{:S(2)}, u32[]{:S(2)}) async-start(bf16[8,2,128,256]{3,2,1,0:T(8,128)(2,1)} %copy.57), calls=%async_computation.1 | async-start | bytes 2097152 | tf_op jit(solution)/shard_map/all_to_all | solution.py:34
  31.9 2.9 %copy-start.1 = (f32[256,1792]{1,0:T(8,128)S(1)}, f32[256,1792]{1,0:T(8,128)}, u32[]{:S(2)}) copy-start(f32[256,1792]{1,0:T(8,128)} %param.17) | copy-start | bytes 5505028
  34.7 1.7 copy-start.4
  61.3 76.0 %copy-start.3 = (bf16[8,2,128,256]{3,2,1,0:T(8,128)(2,1)}, bf16[8,2,128,256]{3,2,1,0:T(8,128)(2,1)S(1)}, u32[]{:S(2)}) copy-start(bf16[8,2,128,256]{3,2,1,0:T(8,128)(2,1)S(1)} %all-to-all-done.1) | copy-start | bytes 3145732
  149.7 5.4 %copy-start.5 = (s32[256]{0:T(256)S(1)}, s32[256]{0:T(256)}, u32[]{:S(2)}) copy-start(s32[256]{0:T(256)} %param.15) | copy-start | bytes 3076
  150.8 28.6 %all-to-all-start.2 = ((bf16[256,16,112]{0,2,1:T(8,128)(2,1)}), bf16[256,16,112]{0,2,1:T(8,128)(2,1)S(1)}, u32[]{:S(2)}, u32[]{:S(2)}) async-start(bf16[256,16,112]{0,2,1:T(8,128)(2,1)} %select_bitcast_fusion), calls=%async_computation.2 | async-start | bytes 1835008 | tf_op jit(solution)/shard_map/all_to_all | solution.py:81
Sparse Core Ops, SparseCore 0:
  11.7 125.5 all-gather.1
where the time goes:
time: 189 us; the launch traced here: 188 us
  waiting for transfers between devices  109 us (58%)
  local copies, waits for them, and re-layouts  22 us (12%)
  between operations  14.9 us (8%)
  starting transfers between devices  13.3 us (7%)
  other arithmetic  11.1 us (6%)
  matrix products  10.6 us (6%)
  blocking collectives  7.4 us (4%)
    all_gather x1, waiting for transfers between devices, on_device(): lax.all_gather(masked, DP, axis=0, tiled=True)  76 us
    all_to_all x1, waiting for transfers between devices, exchange_in_order(): out = lax.all_to_all(out, axes[k], k, k, tiled=True)  19.8 us
    unnamed x21, local copies, waits for them, and re-layouts  16.7 us
    all_to_all x1, waiting for transfers between devices, on_device(): lax.all_to_all(outgoing, 'expert', split_axis=1, concat_axis=1, tiled=True)  13.3 us
    dot_general x1, matrix products, on_device(): lax.dot_general(sliced, lax.all_gather(masked, DP, axis=0, tiled=True), c...  10.6 us
    all_to_all x1, starting transfers between devices, exchange_in_order(): out = lax.all_to_all(out, axes[k], k, k, tiled=True)  8.94 us
    all_to_all x1, blocking collectives, exchange_in_order(): out = lax.all_to_all(out, axes[k], k, k, tiled=True)  7.4 us
    all_to_all x1, starting transfers between devices, on_device(): lax.all_to_all(outgoing, 'expert', split_axis=1, concat_axis=1, tiled=True)  4.34 us
  transfers between devices with their start and end apart: 3, of which 3 were waited for; matrix products, arithmetic and copies ran while one was open for 13% of the time, Pallas kernels for 0%

commit v1 on v0

v1 whole, which is shorter than its diff:
```python
import jax
import jax.numpy as jnp
from jax import lax
from jax.experimental import pallas as pl
from jax.experimental.pallas import tpu as pltpu
from jax.sharding import PartitionSpec as P

MESH = pl.DeviceIdType.MESH
FF = 14336
D = 4096
COLS = 1792
UNIT = 112
GROUPS = 16
HALF_UNITS = FF // UNIT
TOK = 128
CHUNKS = 4
CROWS = TOK // CHUNKS
WIDTH = 256
TILE = 256

beta_one = 0.9
beta_two = 0.95
learn_rate = 0.01
decay_rate = 0.1
epsilon = 1e-08
step_count = 100.0


def dp_of(x, plane, core):
    return (lax.rem(x + 4, 4) * 2 + plane) * 2 + core


def gather_kernel(
    hid_ref, og_ref, rexp_ref, lrow_ref, rrow_ref, count_ref, lsm_ref, rsm_ref,
    grad_ref, index_ref,
    hid, og, abuf, bbuf, abuf_t,
    load_sem, a_send, a_recv, z_send, z_recv, x_send, x_recv, o_send, o_recv, s_send, s_recv,
):
    dp = lax.axis_index("dp")
    ex = lax.axis_index("expert")
    core = lax.rem(dp, 2)
    plane = lax.rem(dp // 2, 2)
    x = dp // 4
    planes = (plane, 1 - plane)

    load_h = pltpu.make_async_copy(hid_ref, hid, load_sem.at[0])
    load_o = pltpu.make_async_copy(og_ref, og, load_sem.at[1])
    load_h.start()
    load_o.start()
    barrier = pltpu.get_barrier_semaphore()
    for k in range(1, 16):
        pl.semaphore_signal(barrier, inc=1, device_id=(lax.rem(dp + k, 16), ex), device_id_type=MESH)

    lane = lax.broadcasted_iota(jnp.int32, (8, COLS), 1)
    unit_of = jnp.zeros((8, COLS), jnp.int32)
    for u in range(GROUPS):
        belongs = (lane >= u * UNIT) & (lane < (u + 1) * UNIT)
        unit_of = jnp.where(belongs, lsm_ref[ex * GROUPS + u], unit_of)
    expert_of = jnp.where(unit_of >= HALF_UNITS, 1, 0)[0:1, :]
    rows = lax.broadcasted_iota(jnp.int32, (TOK, TOK), 0)
    cols = lax.broadcasted_iota(jnp.int32, (TOK, TOK), 1)
    row_expert = jnp.sum(jnp.where(rows == cols, rexp_ref[...], 0), axis=1, keepdims=True)
    live = lax.broadcasted_iota(jnp.int32, (TOK, 1), 0) < count_ref[0, 0]
    row_key = jnp.where(live, row_expert, -1)
    load_h.wait()
    for j in range(CHUNKS):
        key = row_key[j * CROWS : (j + 1) * CROWS]
        kept = key == expert_of
        block = hid[j * CROWS : (j + 1) * CROWS, :].astype(jnp.float32)
        bbuf[plane, j, x * 2 + core] = jnp.where(kept, block, 0.0).astype(jnp.bfloat16)

    wide = lax.broadcasted_iota(jnp.int32, (GROUPS, 256), 1) // GROUPS
    high = lax.broadcasted_iota(jnp.int32, (GROUPS, 1), 0)
    held = jnp.zeros((GROUPS, 1), jnp.int32)
    wanted = jnp.zeros((GROUPS, 1), jnp.int32)
    for u in range(GROUPS):
        held = jnp.where(high == u, lsm_ref[ex * GROUPS + u], held)
        wanted = jnp.where(high == u, rsm_ref[ex * GROUPS + u], wanted)
    target = jnp.sum(jnp.where(rrow_ref[...] == held, wide, 0), axis=1, keepdims=True)
    source = jnp.sum(jnp.where(lrow_ref[...] == wanted, wide, 0), axis=1, keepdims=True)
    low = lax.broadcasted_iota(jnp.int32, (GROUPS, 128), 1)
    high = lax.broadcasted_iota(jnp.int32, (GROUPS, 128), 0)
    order_row = jnp.sum(jnp.where(target == low, high, 0), axis=0, keepdims=True)
    source_row = jnp.sum(jnp.where(high == low, source, 0), axis=0, keepdims=True)
    index_ref[0:1, :] = order_row
    index_ref[1:2, :] = source_row

    load_o.wait()
    pl.semaphore_wait(barrier, 15)

    started = []

    def send(src, dst, ssem, rsem, target_dp):
        copy = pltpu.make_async_remote_copy(
            src_ref=src, dst_ref=dst, send_sem=ssem, recv_sem=rsem,
            device_id=(target_dp, ex), device_id_type=MESH,
        )
        copy.start()
        started.append(copy)

    def arrived(ref, rsem):
        pltpu.make_async_copy(ref, ref, rsem).wait()

    def send_a(other):
        cut = og.at[:, :, pl.ds(pl.multiple_of(other * WIDTH, WIDTH), WIDTH)]
        send(cut, abuf.at[plane, :, x * 2 + core], a_send.at[other], a_recv.at[dp], other)

    for dx in (0, 1, 3, 2):
        for dc in range(2):
            send_a(dp_of(x + dx, 1 - plane, lax.rem(core + dc, 2)))

    def slot(p, j, dx, c):
        return bbuf.at[planes[p], j, lax.rem(x + dx + 4, 4) * 2 + c]

    def center(p, j):
        me = slot(p, j, 0, core)
        send(me, me, x_send.at[p, j, 0], x_recv.at[p, j, 0], dp_of(x + 1, plane, core))
        send(me, me, x_send.at[p, j, 1], x_recv.at[p, j, 1], dp_of(x - 1, plane, core))
        send(me, me, s_send.at[p, j, 0], s_recv.at[p, j, 0], dp_of(x, plane, 1 - core))

    def z_out(j):
        me = slot(0, j, 0, core)
        send(me, me, z_send.at[j], z_recv.at[j], dp_of(x, 1 - plane, core))

    def z_in(j):
        arrived(slot(1, j, 0, core), z_recv.at[j])
        center(1, j)

    def sides(p, j):
        left = slot(p, j, -1, core)
        arrived(left, x_recv.at[p, j, 0])
        first = left.at[pl.ds(0, CROWS // 2)]
        send(first, first, o_send.at[p, j, 0], o_recv.at[p, j, 0], dp_of(x + 1, plane, core))
        send(left, left, s_send.at[p, j, 1], s_recv.at[p, j, 1], dp_of(x, plane, 1 - core))
        right = slot(p, j, 1, core)
        arrived(right, x_recv.at[p, j, 1])
        second = right.at[pl.ds(CROWS // 2, CROWS // 2)]
        send(second, second, o_send.at[p, j, 1], o_recv.at[p, j, 1], dp_of(x - 1, plane, core))
        send(right, right, s_send.at[p, j, 2], s_recv.at[p, j, 2], dp_of(x, plane, 1 - core))

    def opposite(p, j):
        far = slot(p, j, 2, core)
        arrived(far.at[pl.ds(0, CROWS // 2)], o_recv.at[p, j, 0])
        arrived(far.at[pl.ds(CROWS // 2, CROWS // 2)], o_recv.at[p, j, 1])
        send(far, far, s_send.at[p, j, 3], s_recv.at[p, j, 3], dp_of(x, plane, 1 - core))

    def wait_a(p):
        for dx in range(4):
            for dc in range(2):
                if (p, dx, dc) == (0, 0, 0):
                    continue
                c = lax.rem(core + dc, 2)
                src = dp_of(x + dx, planes[p], c)
                arrived(abuf.at[planes[p], :, lax.rem(x + dx, 4) * 2 + c], a_recv.at[src])

    def compute(p, j):
        for i, dx in enumerate((0, -1, 1, 2)):
            arrived(slot(p, j, dx, 1 - core), s_recv.at[p, j, i])
        lhs = abuf[planes[p], j].reshape(8 * CROWS, WIDTH)
        abuf_t[...] = jnp.transpose(lhs)

        def tile(t, carry):
            at = pl.ds(pl.multiple_of(t * TILE, TILE), TILE)
            rhs = bbuf[planes[p], j, :, :, at].reshape(8 * CROWS, TILE)
            part = jnp.dot(abuf_t[...], rhs, preferred_element_type=jnp.float32)
            if (p, j) == (0, 0):
                grad_ref[:, at] = part
            else:
                grad_ref[:, at] += part
            return carry

        lax.fori_loop(0, COLS // TILE, tile, 0)

    for j in range(CHUNKS):
        z_out(j)
        center(0, j)
    for dx in (1, 3, 2, 0):
        for dc in range(2):
            if (dx, dc) != (0, 0):
                send_a(dp_of(x + dx, plane, lax.rem(core + dc, 2)))
    cols_own = pl.ds(pl.multiple_of(dp * WIDTH, WIDTH), WIDTH)
    for j in range(CHUNKS):
        abuf[plane, j, x * 2 + core] = og[j, :, cols_own]

    blocks = [(p, j) for p in range(2) for j in range(CHUNKS)]
    n = len(blocks)
    for i in range(n + 2):
        if i < n:
            sides(*blocks[i])
        if 1 <= i <= n:
            opposite(*blocks[i - 1])
        if i >= 2:
            if i - 2 == 0:
                wait_a(0)
            if i - 2 == CHUNKS:
                wait_a(1)
            compute(*blocks[i - 2])
        if i + 1 < n and blocks[i + 1][0] == 1:
            z_in(blocks[i + 1][1])
    for copy in started:
        copy.wait_send()


def gather_call(hidden, outgrad, row_expert, counts, learner_map, rollout_map):
    vmem = pl.BlockSpec(memory_space=pltpu.VMEM)
    smem = pl.BlockSpec(memory_space=pltpu.SMEM)
    hbm = pl.BlockSpec(memory_space=pl.ANY)
    dma = pltpu.SemaphoreType.DMA
    return pl.pallas_call(
        gather_kernel,
        name="gather_multiply",
        out_shape=(
            jax.ShapeDtypeStruct((WIDTH, COLS), jnp.float32),
            jax.ShapeDtypeStruct((2, 128), jnp.int32),
        ),
        in_specs=[hbm, hbm, vmem, vmem, vmem, smem, smem, smem],
        out_specs=(vmem, vmem),
        scratch_shapes=[
            pltpu.VMEM((TOK, COLS), jnp.bfloat16),
            pltpu.VMEM((CHUNKS, CROWS, D), jnp.bfloat16),
            pltpu.VMEM((2, CHUNKS, 8, CROWS, WIDTH), jnp.bfloat16),
            pltpu.VMEM((2, CHUNKS, 8, CROWS, COLS), jnp.bfloat16),
            pltpu.VMEM((WIDTH, 8 * CROWS), jnp.bfloat16),
            dma((3,)),
            dma((16,)), dma((16,)),
            dma((CHUNKS,)), dma((CHUNKS,)),
            dma((2, CHUNKS, 2)), dma((2, CHUNKS, 2)),
            dma((2, CHUNKS, 2)), dma((2, CHUNKS, 2)),
            dma((2, CHUNKS, 4)), dma((2, CHUNKS, 4)),
        ],
        compiler_params=pltpu.CompilerParams(
            collective_id=0, has_side_effects=True, vmem_limit_bytes=32 * 1024 * 1024
        ),
    )(
        hidden,
        outgrad.reshape(CHUNKS, CROWS, D),
        row_expert,
        learner_map.reshape(1, 256),
        rollout_map.reshape(1, 256),
        counts,
        learner_map,
        rollout_map,
    )


PACKED = 224
FOLD = 32
LANES = 128


def spread_kernel(index_ref, val_ref, out_ref, packed, sends, recvs, send_sem, recv_sem):
    dp = lax.axis_index("dp")
    ex = lax.axis_index("expert")
    barrier = pltpu.get_barrier_semaphore()
    for k in range(1, GROUPS):
        pl.semaphore_signal(
            barrier, inc=1, device_id=(dp, lax.rem(ex + k, GROUPS)), device_id_type=MESH
        )
    lane = lax.broadcasted_iota(jnp.int32, (FOLD, LANES), 1)
    lane_all = lax.broadcasted_iota(jnp.int32, (WIDTH, LANES), 1)

    def shifted(value, by):
        by = by % LANES
        return value if by == 0 else pltpu.roll(value, by, 1)

    for u in range(GROUPS):
        block, off = divmod(u * UNIT, LANES)
        one = shifted(val_ref[:, block * LANES : (block + 1) * LANES], -off)
        if off + UNIT > LANES:
            two = shifted(val_ref[:, (block + 1) * LANES : (block + 2) * LANES], -off)
            one = jnp.where(lane_all < LANES - off, one, two)
        last = one[PACKED:]
        for g in range(PACKED // FOLD):
            extra = shifted(last, UNIT - 16 * g)
            mine = one[g * FOLD : (g + 1) * FOLD]
            packed[u, g * FOLD : (g + 1) * FOLD, :] = jnp.where(lane < UNIT, mine, extra)

    def to_slot(k, carry):
        sends[k] = packed[index_ref[0, lax.rem(ex + k, GROUPS)]]
        return carry

    lax.fori_loop(0, GROUPS, to_slot, 0)
    pl.semaphore_wait(barrier, GROUPS - 1)
    copies = []
    for k in range(1, GROUPS):
        to = lax.rem(ex + k, GROUPS)
        copy = pltpu.make_async_remote_copy(
            src_ref=sends.at[k], dst_ref=recvs.at[ex],
            send_sem=send_sem.at[k], recv_sem=recv_sem.at[k],
            device_id=(dp, to), device_id_type=MESH,
        )
        copy.start()
        copies.append(copy)
    recvs[ex] = sends[0]
    for k in range(1, GROUPS):
        came = recvs.at[lax.rem(ex - k + GROUPS, GROUPS)]
        pltpu.make_async_copy(came, came, recv_sem.at[k]).wait()

    def unfolded(p):
        data = recvs[index_ref[1, p]]
        tail = jnp.zeros((FOLD, LANES), data.dtype)
        for g in range(PACKED // FOLD):
            moved = shifted(data[g * FOLD : (g + 1) * FOLD], 16 * g - UNIT)
            tail = jnp.where((lane >= 16 * g) & (lane < 16 * g + 16), moved, tail)
        return jnp.concatenate([data, tail], axis=0)

    held = unfolded(0)
    pos = 0
    for q in range(COLS // LANES):
        off = q * LANES - pos * UNIT
        nxt = unfolded(pos + 1)
        a = shifted(held, -off)
        b = shifted(nxt, UNIT - off)
        out_ref[:, q * LANES : (q + 1) * LANES] = jnp.where(lane_all < UNIT - off, a, b)
        pos += 1
        held = nxt
        if (q + 1) * LANES - pos * UNIT == UNIT and pos + 1 < GROUPS:
            pos += 1
            held = unfolded(pos)
    for copy in copies:
        copy.wait_send()


def spread_call(index, value):
    vmem = pl.BlockSpec(memory_space=pltpu.VMEM)
    dma = pltpu.SemaphoreType.DMA
    return pl.pallas_call(
        spread_kernel,
        name="spread_units",
        out_shape=jax.ShapeDtypeStruct((WIDTH, COLS), jnp.bfloat16),
        in_specs=[pl.BlockSpec(memory_space=pltpu.SMEM), vmem],
        out_specs=vmem,
        scratch_shapes=[
            pltpu.VMEM((GROUPS, PACKED, LANES), jnp.bfloat16),
            pltpu.VMEM((GROUPS, PACKED, LANES), jnp.bfloat16),
            pltpu.VMEM((GROUPS, PACKED, LANES), jnp.bfloat16),
            dma((GROUPS,)), dma((GROUPS,)),
        ],
        compiler_params=pltpu.CompilerParams(
            collective_id=1, has_side_effects=True, vmem_limit_bytes=16 * 1024 * 1024
        ),
    )(index, value)


def on_device(
    hidden, outgrad, row_expert, counts, learner_map, rollout_map, master, moment1, moment2
):
    gradient, index = gather_call(
        hidden[0], outgrad[0], row_expert, counts, learner_map, rollout_map
    )
    new_moment1 = beta_one * moment1 + (1.0 - beta_one) * gradient
    new_moment2 = beta_two * moment2 + (1.0 - beta_two) * gradient * gradient
    bias_one = 1.0 - beta_one**step_count
    bias_two = 1.0 - beta_two**step_count
    update = new_moment1 / bias_one / (jnp.sqrt(new_moment2 / bias_two) + epsilon)
    new_master = master - learn_rate * (update + decay_rate * master)
    rollout_weights = spread_call(index, new_master.astype(jnp.bfloat16))
    return (new_master, new_moment1, new_moment2, rollout_weights)


def solution(mesh):
    return jax.shard_map(
        on_device,
        mesh=mesh,
        in_specs=(
            P("expert", "dp", None),
            P("expert", "dp", None),
            P("expert", "dp"),
            P("expert", "dp"),
            P(),
            P(),
            P("dp", "expert"),
            P("dp", "expert"),
            P("dp", "expert"),
        ),
        out_specs=(P("dp", "expert"),) * 4,
        check_vma=False,
    )
```

time: 189 us -> 117 us (0.62)
  waiting for transfers between devices: 109 us -> 0 us
  Pallas kernels: 0 us -> 103 us
  local copies, waits for them, and re-layouts: 22 us -> 5.17 us
  between operations: 14.9 us -> 1.31 us
  starting transfers between devices: 13.3 us -> 0 us
  matrix products: 10.6 us -> 0 us
  blocking collectives: 7.4 us -> 0 us
  other arithmetic: 11.1 us -> 5.95 us
    pallas_call x0 -> x2, Pallas kernels: none -> 103 us  [the longest x1 72.5 us: gather_call(): pl.pallas_call(gather_kernel, name='gather_multiply', out_shape=(jax.Shap...]
    all_gather x1 -> x0, waiting for transfers between devices: 76 us -> none  [on_device(): lax.all_gather(masked, DP, axis=0, tiled=True)]
    all_to_all x2 -> x0, waiting for transfers between devices: 33.1 us -> none  [the longest x1 19.8 us: exchange_in_order(): out = lax.all_to_all(out, axes[k], k, k, tiled=True)]
    all_to_all x2 -> x0, starting transfers between devices: 13.3 us -> none  [the longest x1 8.94 us: exchange_in_order(): out = lax.all_to_all(out, axes[k], k, k, tiled=True)]
    unnamed x21 -> x11, local copies, waits for them, and re-layouts: 16.7 us -> 5.17 us
    dot_general x1 -> x0, matrix products: 10.6 us -> none  [on_device(): lax.dot_general(sliced, lax.all_gather(masked, DP, axis=0, tiled=True), c...]
    sort x3 -> x0, other arithmetic: 7.51 us -> none  [the longest x1 3.17 us: on_device(): inverse_learn = jnp.argsort(learner_map)]
    all_to_all x1 -> x0, blocking collectives: 7.4 us -> none  [exchange_in_order(): out = lax.all_to_all(out, axes[k], k, k, tiled=True)]
  transfers between devices with their start and end apart: 3 -> 0, of which waited for: 3 -> 0; matrix products, arithmetic and copies ran while one was open for 13% -> 0% of each run, Pallas kernels for 0% -> 0%
where the time goes in v1:
time: 117 us; the launch traced here: 115 us
  Pallas kernels  103 us (88%)
  other arithmetic  5.95 us (5%)
  local copies, waits for them, and re-layouts  5.17 us (4%)
  between operations  1.31 us (1%)
    pallas_call x1, Pallas kernels, gather_call(): pl.pallas_call(gather_kernel, name='gather_multiply', out_shape=(jax.Shap...  72.5 us
    pallas_call x1, Pallas kernels, spread_call(): pl.pallas_call(spread_kernel, name='spread_units', out_shape=jax.ShapeDty...  30.5 us
    convert_element_type x1, other arithmetic, on_device(): rollout_weights = spread_call(index, new_master.astype(jnp.bfloat16))  5.95 us
    unnamed x11, local copies, waits for them, and re-layouts  5.17 us

profile of v1, /device:TPU:1, one launch (start us, length us, event | category | flops | bytes accessed | tf_op | source)
XLA Modules:
  0.0 115.4 jit_solution(9585841774172978118)
XLA Ops:
  1.3 0.0 copy-start
  1.3 1.2 %copy-done = bf16[1,128,4096]{2,1,0:T(8,128)(2,1)S(1)} copy-done((bf16[1,128,4096]{2,1,0:T(8,128)(2,1)S(1)}, bf16[1,128,4096]{2,1,0:T(8,128)(2,1)}, u32[]{:S(2)}) %copy-start) | copy-done | bytes 1048600
  2.5 0.0 copy-start.1
  2.5 1.0 copy-done.1
  3.5 0.0 copy-start.2
  3.5 0.7 copy-done.2
  4.2 0.0 copy-start.3
  4.2 0.7 copy-done.3
  4.9 0.0 copy-start.4
  4.9 0.7 copy-done.4
  5.5 72.5 %gather_multiply.1 = (f32[256,1792]{1,0:T(8,128)S(1)}, s32[2,128]{1,0:T(2,128)S(1)}) custom-call(bf16[128,1792]{1,0:T(8,128)(2,1)S(1)} %bitcast.5, bf16[4,32,4096]{2,1,0:T(8,128)(2,1)S(1)} %bitcast.4, s32[1,128]{1,0:T(1,128)S(1)} %copy-done.4, s32[1,256]{1,0:T(1,128)S(1)} %bitcast.6, s32[1,256]{1,0:T(1,128)S(1)} %bitcast.7, s32[1,1]{1,0:T(1,128)S(6)} %copy.14.count_ref, ...), custom_call_target="tpu_custom_call" | custom-call | tf_op jit(solution)/shard_map/gather_multiply/pallas_call | solution.py:209
  78.0 5.9 %fusion.1 = (bf16[256,1792]{1,0:T(8,128)(2,1)S(1)}, f32[256,1792]{1,0:T(8,128)}, f32[256,1792]{1,0:T(8,128)}, f32[256,1792]{1,0:T(8,128)}) fusion(f32[256,1792]{1,0:T(8,128)} %param.15, f32[256,1792]{1,0:T(8,128)S(1)} %get-tuple-element.6, f32[256,1792]{1,0:T(8,128)} %param.16, f32[256,1792]{1,0:T(8,128)} %param.17), kind=kLoop, calls=%fused_computation.4 | loop fusion | flops 7340032 | bytes 13762560 | tf_op jit(solution)/shard_map/convert_element_type | solution.py:357
  84.0 30.5 %spread_units.1 = bf16[256,1792]{1,0:T(8,128)(2,1)S(1)} custom-call(s32[2,128]{1,0:T(2,128)S(1)} %get-tuple-element.7.index_ref, bf16[256,1792]{1,0:T(8,128)(2,1)S(1)} %get-tuple-element.8.val_ref), custom_call_target="tpu_custom_call" | custom-call | tf_op jit(solution)/shard_map/spread_units/pallas_call | solution.py:327
  114.5 0.9 copy.15
Async XLA Ops:
  1.3 1.2 %copy-start = (bf16[1,128,4096]{2,1,0:T(8,128)(2,1)S(1)}, bf16[1,128,4096]{2,1,0:T(8,128)(2,1)}, u32[]{:S(2)}) copy-start(bf16[1,128,4096]{2,1,0:T(8,128)(2,1)} %param.10) | copy-start | bytes 3145732
  2.5 1.0 copy-start.1
  3.5 0.7 copy-start.2
  4.2 0.7 copy-start.3
  4.9 0.7 copy-start.4

commit v2 on v0

v2 whole, which is shorter than its diff:
```python
import jax
import jax.numpy as jnp
from jax import lax
from jax.experimental import pallas as pl
from jax.experimental.pallas import tpu as pltpu
from jax.sharding import PartitionSpec as P

MESH = pl.DeviceIdType.MESH
FF = 14336
D = 4096
COLS = 1792
UNIT = 112
GROUPS = 16
HALF_UNITS = FF // UNIT
TOK = 128
CHUNKS = 4
CROWS = TOK // CHUNKS
WIDTH = 256
TILE = 256
PARTS = 2
DROWS = WIDTH // PARTS
FOLD = 16
PACKED = DROWS - FOLD
LANES = 128

beta_one = 0.9
beta_two = 0.95
learn_rate = 0.01
decay_rate = 0.1
epsilon = 1e-08
step_count = 100.0


def dp_of(x, plane, core):
    return (lax.rem(x + 4, 4) * 2 + plane) * 2 + core


def step_kernel(
    hid_ref, og_ref, rexp_ref, lrow_ref, rrow_ref, count_ref, lsm_ref, rsm_ref,
    master_ref, mom1_ref, mom2_ref,
    new_master, new_mom1, new_mom2, out_ref,
    hid, og, rexp, lrow, rrow, master, mom1, mom2, abuf, bbuf, lhs_t, grad,
    index_v, index, value, packed, sends, recv_0, recv_1,
    load_sem, a_send, a_recv, z_send, z_recv, x_send, x_recv, o_send, o_recv, s_send, s_recv,
    e_send, e_recv,
):
    recvs = (recv_0, recv_1)
    dp = lax.axis_index("dp")
    ex = lax.axis_index("expert")
    core = lax.rem(dp, 2)
    plane = lax.rem(dp // 2, 2)
    x = dp // 4
    planes = (plane, 1 - plane)

    loads = [
        pltpu.make_async_copy(src, dst, load_sem.at[i])
        for i, (src, dst) in enumerate(
            (
                (hid_ref, hid), (rexp_ref, rexp), (lrow_ref, lrow), (rrow_ref, rrow), (og_ref, og),
                (mom1_ref, mom1), (mom2_ref, mom2), (master_ref, master),
            )
        )
    ]
    for load in loads:
        load.start()
    barrier = pltpu.get_barrier_semaphore()
    for k in range(1, 16):
        pl.semaphore_signal(barrier, inc=1, device_id=(lax.rem(dp + k, 16), ex), device_id_type=MESH)
    for k in range(1, 16):
        pl.semaphore_signal(barrier, inc=1, device_id=(dp, lax.rem(ex + k, 16)), device_id_type=MESH)

    lane = lax.broadcasted_iota(jnp.int32, (8, COLS), 1)
    unit_of = jnp.zeros((8, COLS), jnp.int32)
    for u in range(GROUPS):
        belongs = (lane >= u * UNIT) & (lane < (u + 1) * UNIT)
        unit_of = jnp.where(belongs, lsm_ref[ex * GROUPS + u], unit_of)
    expert_of = jnp.where(unit_of >= HALF_UNITS, 1, 0)[0:1, :]
    rows = lax.broadcasted_iota(jnp.int32, (TOK, TOK), 0)
    cols = lax.broadcasted_iota(jnp.int32, (TOK, TOK), 1)
    for load in loads[:4]:
        load.wait()
    row_expert = jnp.sum(jnp.where(rows == cols, rexp[...], 0), axis=1, keepdims=True)
    live = lax.broadcasted_iota(jnp.int32, (TOK, 1), 0) < count_ref[0, 0]
    row_key = jnp.where(live, row_expert, -1)
    for j in range(CHUNKS):
        key = row_key[j * CROWS : (j + 1) * CROWS]
        kept = key == expert_of
        block = hid[j * CROWS : (j + 1) * CROWS, :].astype(jnp.float32)
        bbuf[plane, j, x * 2 + core] = jnp.where(kept, block, 0.0).astype(jnp.bfloat16)
    loads[4].wait()
    pl.semaphore_wait(barrier, 30)

    started = []

    def send(src, dst, ssem, rsem, to):
        copy = pltpu.make_async_remote_copy(
            src_ref=src, dst_ref=dst, send_sem=ssem, recv_sem=rsem,
            device_id=to, device_id_type=MESH,
        )
        copy.start()
        started.append(copy)

    def arrived(ref, rsem):
        pltpu.make_async_copy(ref, ref, rsem).wait()

    def a_columns(k, other):
        return pl.ds(pl.multiple_of(other * WIDTH + k * DROWS, DROWS), DROWS)

    def send_a(k, other):
        cut = og.at[:, :, a_columns(k, other)]
        slot_a = abuf.at[k, plane, :, x * 2 + core]
        send(cut, slot_a, a_send.at[k, other], a_recv.at[k, dp], (other, ex))

    def all_a(k):
        for dx in (0, 1, 3, 2):
            for dc in range(2):
                c = lax.rem(core + dc, 2)
                send_a(k, dp_of(x + dx, 1 - plane, c))
                if (dx, dc) != (0, 0):
                    send_a(k, dp_of(x + dx, plane, c))

    def slot(p, j, dx, c):
        return bbuf.at[planes[p], j, lax.rem(x + dx + 4, 4) * 2 + c]

    def peer(dx, c):
        return (dp_of(x + dx, plane, c), ex)

    def center(p, j):
        me = slot(p, j, 0, core)
        send(me, me, x_send.at[p, j, 0], x_recv.at[p, j, 0], peer(1, core))
        send(me, me, x_send.at[p, j, 1], x_recv.at[p, j, 1], peer(-1, core))
        send(me, me, s_send.at[p, j, 0], s_recv.at[p, j, 0], peer(0, 1 - core))

    def z_out(j):
        me = slot(0, j, 0, core)
        send(me, me, z_send.at[j], z_recv.at[j], (dp_of(x, 1 - plane, core), ex))

    def z_in(j):
        arrived(slot(1, j, 0, core), z_recv.at[j])
        center(1, j)

    def sides(p, j):
        left = slot(p, j, -1, core)
        arrived(left, x_recv.at[p, j, 0])
        first = left.at[pl.ds(0, CROWS // 2)]
        send(first, first, o_send.at[p, j, 0], o_recv.at[p, j, 0], peer(1, core))
        send(left, left, s_send.at[p, j, 1], s_recv.at[p, j, 1], peer(0, 1 - core))
        right = slot(p, j, 1, core)
        arrived(right, x_recv.at[p, j, 1])
        second = right.at[pl.ds(CROWS // 2, CROWS // 2)]
        send(second, second, o_send.at[p, j, 1], o_recv.at[p, j, 1], peer(-1, core))
        send(right, right, s_send.at[p, j, 2], s_recv.at[p, j, 2], peer(0, 1 - core))

    def opposite(p, j):
        far = slot(p, j, 2, core)
        arrived(far.at[pl.ds(0, CROWS // 2)], o_recv.at[p, j, 0])
        arrived(far.at[pl.ds(CROWS // 2, CROWS // 2)], o_recv.at[p, j, 1])
        send(far, far, s_send.at[p, j, 3], s_recv.at[p, j, 3], peer(0, 1 - core))

    def wait_a(k, p):
        for dx in range(4):
            for dc in range(2):
                if (p, dx, dc) == (0, 0, 0):
                    continue
                c = lax.rem(core + dc, 2)
                src = dp_of(x + dx, planes[p], c)
                arrived(abuf.at[k, planes[p], :, lax.rem(x + dx, 4) * 2 + c], a_recv.at[k, src])

    def wait_sibling(p):
        for j in range(CHUNKS):
            for i, dx in enumerate((0, -1, 1, 2)):
                arrived(slot(p, j, dx, 1 - core), s_recv.at[p, j, i])

    def multiply(k, p):
        lhs = abuf[k, planes[p]].reshape(8 * TOK, DROWS)
        lhs_t[...] = jnp.transpose(lhs)

        def tile(t, carry):
            at = pl.ds(pl.multiple_of(t * TILE, TILE), TILE)
            rhs = bbuf[planes[p], :, :, :, at].reshape(8 * TOK, TILE)
            part = jnp.dot(lhs_t[...], rhs, preferred_element_type=jnp.float32)
            if p == 0:
                grad[:, at] = part
            else:
                grad[:, at] += part
            return carry

        lax.fori_loop(0, COLS // TILE, tile, 0)

    bias_one = 1.0 - beta_one**step_count
    bias_two = 1.0 - beta_two**step_count

    def update(k):
        def piece(i, carry):
            r = pl.multiple_of(lax.rem(i, DROWS // 32) * 32, 32)
            at = pl.ds(pl.multiple_of((i // (DROWS // 32)) * TILE, TILE), TILE)
            here = (pl.ds(k * DROWS + r, 32), at)
            g = grad[pl.ds(r, 32), at]
            m1 = beta_one * mom1[here] + (1.0 - beta_one) * g
            m2 = beta_two * mom2[here] + (1.0 - beta_two) * g * g
            w = master[here]
            step = m1 * (1.0 / bias_one) / (jnp.sqrt(m2 * (1.0 / bias_two)) + epsilon)
            w = w - learn_rate * (step + decay_rate * w)
            new_mom1[here] = m1
            new_mom2[here] = m2
            new_master[here] = w
            value[pl.ds(r, 32), at] = w.astype(jnp.bfloat16)
            return carry

        lax.fori_loop(0, (DROWS // 32) * (COLS // TILE), piece, 0)

    lane_fold = lax.broadcasted_iota(jnp.int32, (FOLD, LANES), 1)
    lane_all = lax.broadcasted_iota(jnp.int32, (DROWS, LANES), 1)

    def shifted(val, by):
        by = by % LANES
        return val if by == 0 else pltpu.roll(val, by, 1)

    def pack():
        for u in range(GROUPS):
            block, off = divmod(u * UNIT, LANES)
            one = shifted(value[:, block * LANES : (block + 1) * LANES], -off)
            if off + UNIT > LANES:
                two = shifted(value[:, (block + 1) * LANES : (block + 2) * LANES], -off)
                one = jnp.where(lane_all < LANES - off, one, two)
            last = one[PACKED:]
            for g in range(PACKED // FOLD):
                extra = shifted(last, UNIT - 16 * g)
                mine = one[g * FOLD : (g + 1) * FOLD]
                packed[u, g * FOLD : (g + 1) * FOLD, :] = jnp.where(lane_fold < UNIT, mine, extra)

    def spread(k):
        def to_slot(i, carry):
            sends[k, i] = packed[index[0, lax.rem(ex + i, GROUPS)]]
            return carry

        lax.fori_loop(0, GROUPS, to_slot, 0)
        for i in range(1, GROUPS):
            to = lax.rem(ex + i, GROUPS)
            send(sends.at[k, i], recvs[k].at[ex], e_send.at[k, i], e_recv.at[k, i], (dp, to))
        recvs[k][ex] = sends[k, 0]

    def collect(k):
        for i in range(1, GROUPS):
            arrived(recvs[k].at[lax.rem(ex - i + GROUPS, GROUPS)], e_recv.at[k, i])

        def unfolded(p):
            data = recvs[k][index[1, p]]
            tail = jnp.zeros((FOLD, LANES), data.dtype)
            for g in range(PACKED // FOLD):
                moved = shifted(data[g * FOLD : (g + 1) * FOLD], 16 * g - UNIT)
                tail = jnp.where((lane_fold >= 16 * g) & (lane_fold < 16 * g + 16), moved, tail)
            return jnp.concatenate([data, tail], axis=0)

        held = unfolded(0)
        pos = 0
        for q in range(COLS // LANES):
            off = q * LANES - pos * UNIT
            nxt = unfolded(pos + 1)
            a = shifted(held, -off)
            b = shifted(nxt, UNIT - off)
            joined = jnp.where(lane_all < UNIT - off, a, b)
            out_ref[k * DROWS : (k + 1) * DROWS, q * LANES : (q + 1) * LANES] = joined
            pos += 1
            held = nxt
            if (q + 1) * LANES - pos * UNIT == UNIT and pos + 1 < GROUPS:
                pos += 1
                held = unfolded(pos)

    for j in range(CHUNKS):
        z_out(j)
        center(0, j)
    all_a(0)
    for k in range(PARTS):
        for j in range(CHUNKS):
            abuf[k, plane, j, x * 2 + core] = og[j, :, a_columns(k, dp)]

    wide = lax.broadcasted_iota(jnp.int32, (GROUPS, 256), 1) // GROUPS
    high = lax.broadcasted_iota(jnp.int32, (GROUPS, 1), 0)
    have = jnp.zeros((GROUPS, 1), jnp.int32)
    wanted = jnp.zeros((GROUPS, 1), jnp.int32)
    for u in range(GROUPS):
        have = jnp.where(high == u, lsm_ref[ex * GROUPS + u], have)
        wanted = jnp.where(high == u, rsm_ref[ex * GROUPS + u], wanted)
    target = jnp.max(jnp.where(rrow[...] == have, wide, 0), axis=1, keepdims=True)
    source = jnp.max(jnp.where(lrow[...] == wanted, wide, 0), axis=1, keepdims=True)
    low = lax.broadcasted_iota(jnp.int32, (GROUPS, 128), 1)
    high = lax.broadcasted_iota(jnp.int32, (GROUPS, 128), 0)
    index_v[0:1, :] = jnp.max(jnp.where(target == low, high, 0), axis=0, keepdims=True)
    index_v[1:2, :] = jnp.max(jnp.where(high == low, source, 0), axis=0, keepdims=True)
    to_scalar = pltpu.make_async_copy(index_v, index, load_sem.at[8])

    sides(0, 0)
    sides(0, 1)
    to_scalar.start()
    z_in(0)
    sides(0, 2)
    sides(0, 3)
    z_in(1)
    opposite(0, 0)
    opposite(0, 1)
    z_in(2)
    opposite(0, 2)
    opposite(0, 3)
    sides(1, 0)
    z_in(3)
    all_a(1)
    sides(1, 1)
    sides(1, 2)
    sides(1, 3)
    to_scalar.wait()
    for load in loads[5:]:
        load.wait()
    wait_sibling(0)
    wait_a(0, 0)
    multiply(0, 0)
    for j in range(CHUNKS):
        opposite(1, j)
    wait_sibling(1)
    wait_a(0, 1)
    multiply(0, 1)
    update(0)
    pack()
    spread(0)
    wait_a(1, 0)
    multiply(1, 0)
    wait_a(1, 1)
    multiply(1, 1)
    update(1)
    pack()
    spread(1)
    collect(0)
    collect(1)
    for copy in started:
        copy.wait_send()


def step_call(hidden, outgrad, row_expert, counts, learner_map, rollout_map, master, mom1, mom2):
    vmem = pl.BlockSpec(memory_space=pltpu.VMEM)
    smem = pl.BlockSpec(memory_space=pltpu.SMEM)
    hbm = pl.BlockSpec(memory_space=pltpu.HBM)
    dma = pltpu.SemaphoreType.DMA
    state = pltpu.VMEM((WIDTH, COLS), jnp.float32)

    def far(value):
        return pltpu.with_memory_space_constraint(value, pltpu.HBM)

    return pl.pallas_call(
        step_kernel,
        name="grad_update_spread",
        out_shape=(state, state, state, pltpu.VMEM((WIDTH, COLS), jnp.bfloat16)),
        in_specs=[hbm, hbm, hbm, hbm, hbm, smem, smem, smem, hbm, hbm, hbm],
        out_specs=(vmem, vmem, vmem, vmem),
        scratch_shapes=[
            pltpu.VMEM((TOK, COLS), jnp.bfloat16),
            pltpu.VMEM((CHUNKS, CROWS, D), jnp.bfloat16),
            pltpu.VMEM((1, TOK), jnp.int32),
            pltpu.VMEM((1, 256), jnp.int32),
            pltpu.VMEM((1, 256), jnp.int32),
            pltpu.VMEM((WIDTH, COLS), jnp.float32),
            pltpu.VMEM((WIDTH, COLS), jnp.float32),
            pltpu.VMEM((WIDTH, COLS), jnp.float32),
            pltpu.VMEM((PARTS, 2, CHUNKS, 8, CROWS, DROWS), jnp.bfloat16),
            pltpu.VMEM((2, CHUNKS, 8, CROWS, COLS), jnp.bfloat16),
            pltpu.VMEM((DROWS, 8 * TOK), jnp.bfloat16),
            pltpu.VMEM((DROWS, COLS), jnp.float32),
            pltpu.VMEM((2, 128), jnp.int32),
            pltpu.SMEM((2, 128), jnp.int32),
            pltpu.VMEM((DROWS, COLS), jnp.bfloat16),
            pltpu.VMEM((GROUPS, PACKED, LANES), jnp.bfloat16),
            pltpu.VMEM((PARTS, GROUPS, PACKED, LANES), jnp.bfloat16),
            pltpu.VMEM((GROUPS, PACKED, LANES), jnp.bfloat16),
            pltpu.VMEM((GROUPS, PACKED, LANES), jnp.bfloat16),
            dma((9,)),
            dma((PARTS, 16)), dma((PARTS, 16)),
            dma((CHUNKS,)), dma((CHUNKS,)),
            dma((2, CHUNKS, 2)), dma((2, CHUNKS, 2)),
            dma((2, CHUNKS, 2)), dma((2, CHUNKS, 2)),
            dma((2, CHUNKS, 4)), dma((2, CHUNKS, 4)),
            dma((PARTS, GROUPS)), dma((PARTS, GROUPS)),
        ],
        compiler_params=pltpu.CompilerParams(
            collective_id=0, has_side_effects=True, vmem_limit_bytes=40 * 1024 * 1024
        ),
    )(
        far(hidden),
        far(outgrad.reshape(CHUNKS, CROWS, D)),
        far(row_expert),
        far(learner_map.reshape(1, 256)),
        far(rollout_map.reshape(1, 256)),
        counts,
        learner_map,
        rollout_map,
        far(master),
        far(mom1),
        far(mom2),
    )


def land_kernel(*refs):
    ins, outs, sem = refs[:4], refs[4:8], refs[8]
    copies = [pltpu.make_async_copy(a, b, sem.at[i]) for i, (a, b) in enumerate(zip(ins, outs))]
    for copy in copies:
        copy.start()
    for copy in copies:
        copy.wait()


def land_call(values):
    return pl.pallas_call(
        land_kernel,
        name="land_outputs",
        out_shape=tuple(jax.ShapeDtypeStruct(v.shape, v.dtype) for v in values),
        in_specs=[pl.BlockSpec(memory_space=pltpu.VMEM)] * 4,
        out_specs=(pl.BlockSpec(memory_space=pltpu.HBM),) * 4,
        scratch_shapes=[pltpu.SemaphoreType.DMA((4,))],
        compiler_params=pltpu.CompilerParams(vmem_limit_bytes=4 * 1024 * 1024),
    )(*values)


def on_device(
    hidden, outgrad, row_expert, counts, learner_map, rollout_map, master, moment1, moment2
):
    return land_call(
        step_call(
            hidden[0], outgrad[0], row_expert, counts, learner_map, rollout_map,
            master, moment1, moment2,
        )
    )


def solution(mesh):
    return jax.shard_map(
        on_device,
        mesh=mesh,
        in_specs=(
            P("expert", "dp", None),
            P("expert", "dp", None),
            P("expert", "dp"),
            P("expert", "dp"),
            P(),
            P(),
            P("dp", "expert"),
            P("dp", "expert"),
            P("dp", "expert"),
        ),
        out_specs=(P("dp", "expert"),) * 4,
        check_vma=False,
    )
```

time: 189 us -> 89.9 us (0.48)
  waiting for transfers between devices: 109 us -> 0 us
  Pallas kernels: 0 us -> 88.5 us
  local copies, waits for them, and re-layouts: 22 us -> 0 us
  between operations: 14.9 us -> 1.29 us
  starting transfers between devices: 13.3 us -> 0 us
  other arithmetic: 11.1 us -> 0 us
  matrix products: 10.6 us -> 0 us
  blocking collectives: 7.4 us -> 0 us
    pallas_call x0 -> x2, Pallas kernels: none -> 88.5 us  [the longest x1 85.7 us: step_call(): pl.pallas_call(step_kernel, name='grad_update_spread', out_shape=(state,...]
    all_gather x1 -> x0, waiting for transfers between devices: 76 us -> none  [on_device(): lax.all_gather(masked, DP, axis=0, tiled=True)]
    all_to_all x2 -> x0, waiting for transfers between devices: 33.1 us -> none  [the longest x1 19.8 us: exchange_in_order(): out = lax.all_to_all(out, axes[k], k, k, tiled=True)]
    unnamed x21 -> x0, local copies, waits for them, and re-layouts: 16.7 us -> none
    all_to_all x2 -> x0, starting transfers between devices: 13.3 us -> none  [the longest x1 8.94 us: exchange_in_order(): out = lax.all_to_all(out, axes[k], k, k, tiled=True)]
    dot_general x1 -> x0, matrix products: 10.6 us -> none  [on_device(): lax.dot_general(sliced, lax.all_gather(masked, DP, axis=0, tiled=True), c...]
    sort x3 -> x0, other arithmetic: 7.51 us -> none  [the longest x1 3.17 us: on_device(): inverse_learn = jnp.argsort(learner_map)]
    all_to_all x1 -> x0, blocking collectives: 7.4 us -> none  [exchange_in_order(): out = lax.all_to_all(out, axes[k], k, k, tiled=True)]
  transfers between devices with their start and end apart: 3 -> 0, of which waited for: 3 -> 0; matrix products, arithmetic and copies ran while one was open for 13% -> 0% of each run, Pallas kernels for 0% -> 0%
where the time goes in v2:
time: 89.9 us; the launch traced here: 89.8 us
  Pallas kernels  88.5 us (98%)
  between operations  1.29 us (1%)
    pallas_call x1, Pallas kernels, step_call(): pl.pallas_call(step_kernel, name='grad_update_spread', out_shape=(state,...  85.7 us
    pallas_call x1, Pallas kernels, land_call(): pl.pallas_call(land_kernel, name='land_outputs', out_shape=tuple((jax.Sha...  2.77 us

profile of v2, /device:TPU:1, one launch (start us, length us, event | category | flops | bytes accessed | tf_op | source)
XLA Modules:
  0.0 89.8 jit_solution(2787169867493058502)
XLA Ops:
  1.3 85.7 %grad_update_spread.1 = (f32[256,1792]{1,0:T(8,128)S(1)}, f32[256,1792]{1,0:T(8,128)S(1)}, f32[256,1792]{1,0:T(8,128)S(1)}, bf16[256,1792]{1,0:T(8,128)(2,1)S(1)}) custom-call(bf16[128,1792]{1,0:T(8,128)(2,1)} %bitcast.5, bf16[4,32,4096]{2,1,0:T(8,128)(2,1)} %bitcast.4, s32[1,128]{1,0:T(1,128)} %rexp_ref.1, s32[1,256]{1,0:T(1,128)} %bitcast.6, ...), custom_call_target="tpu_custom_call" | custom-call | tf_op jit(solution)/shard_map/grad_update_spread/pallas_call | solution.py:348
  87.0 2.8 %land_outputs.1 = (f32[256,1792]{1,0:T(8,128)}, f32[256,1792]{1,0:T(8,128)}, f32[256,1792]{1,0:T(8,128)}, bf16[256,1792]{1,0:T(8,128)(2,1)}) custom-call(f32[256,1792]{1,0:T(8,128)S(1)} %get-tuple-element.8.refs_0_, f32[256,1792]{1,0:T(8,128)S(1)} %get-tuple-element.9.refs_1_, f32[256,1792]{1,0:T(8,128)S(1)} %get-tuple-element.10.refs_2_, ...), custom_call_target="tpu_custom_call" | custom-call | tf_op jit(solution)/shard_map/land_outputs/pallas_call | solution.py:410

commit v3 on v2

--- a/solution.py
+++ b/solution.py
@@ -36,10 +36,10 @@
 
 
 def step_kernel(
-    hid_ref, og_ref, rexp_ref, lrow_ref, rrow_ref, count_ref, lsm_ref, rsm_ref,
+    hid_ref, og_ref, rexp_ref, lrow_ref, rrow_ref, count_ref,
     master_ref, mom1_ref, mom2_ref,
     new_master, new_mom1, new_mom2, out_ref,
-    hid, og, rexp, lrow, rrow, master, mom1, mom2, abuf, bbuf, lhs_t, grad,
+    hid, og, rexp, lrow, rrow, lsm_ref, rsm_ref, master, mom1, mom2, abuf, bbuf, lhs_t, grad,
     index_v, index, value, packed, sends, recv_0, recv_1,
     load_sem, a_send, a_recv, z_send, z_recv, x_send, x_recv, o_send, o_recv, s_send, s_recv,
     e_send, e_recv,
@@ -52,32 +52,35 @@
     x = dp // 4
     planes = (plane, 1 - plane)
 
+    barrier = pltpu.get_barrier_semaphore()
+    for k in range(1, 16):
+        pl.semaphore_signal(barrier, inc=1, device_id=(lax.rem(dp + k, 16), ex), device_id_type=MESH)
+    for k in range(1, 16):
+        pl.semaphore_signal(barrier, inc=1, device_id=(dp, lax.rem(ex + k, 16)), device_id_type=MESH)
     loads = [
         pltpu.make_async_copy(src, dst, load_sem.at[i])
         for i, (src, dst) in enumerate(
             (
-                (hid_ref, hid), (rexp_ref, rexp), (lrow_ref, lrow), (rrow_ref, rrow), (og_ref, og),
+                (lrow_ref, lsm_ref), (rrow_ref, rsm_ref), (hid_ref, hid), (rexp_ref, rexp), (og_ref, og),
                 (mom1_ref, mom1), (mom2_ref, mom2), (master_ref, master),
+                (lrow_ref, lrow), (rrow_ref, rrow),
             )
         )
     ]
     for load in loads:
         load.start()
-    barrier = pltpu.get_barrier_semaphore()
-    for k in range(1, 16):
-        pl.semaphore_signal(barrier, inc=1, device_id=(lax.rem(dp + k, 16), ex), device_id_type=MESH)
-    for k in range(1, 16):
-        pl.semaphore_signal(barrier, inc=1, device_id=(dp, lax.rem(ex + k, 16)), device_id_type=MESH)
-
+
+    for load in loads[:2]:
+        load.wait()
     lane = lax.broadcasted_iota(jnp.int32, (8, COLS), 1)
     unit_of = jnp.zeros((8, COLS), jnp.int32)
     for u in range(GROUPS):
         belongs = (lane >= u * UNIT) & (lane < (u + 1) * UNIT)
-        unit_of = jnp.where(belongs, lsm_ref[ex * GROUPS + u], unit_of)
+        unit_of = jnp.where(belongs, lsm_ref[0, ex * GROUPS + u], unit_of)
     expert_of = jnp.where(unit_of >= HALF_UNITS, 1, 0)[0:1, :]
     rows = lax.broadcasted_iota(jnp.int32, (TOK, TOK), 0)
     cols = lax.broadcasted_iota(jnp.int32, (TOK, TOK), 1)
-    for load in loads[:4]:
+    for load in loads[2:4]:
         load.wait()
     row_expert = jnp.sum(jnp.where(rows == cols, rexp[...], 0), axis=1, keepdims=True)
     live = lax.broadcasted_iota(jnp.int32, (TOK, 1), 0) < count_ref[0, 0]
@@ -111,13 +114,16 @@
         slot_a = abuf.at[k, plane, :, x * 2 + core]
         send(cut, slot_a, a_send.at[k, other], a_recv.at[k, dp], (other, ex))
 
-    def all_a(k):
+    def a_across(k):
         for dx in (0, 1, 3, 2):
             for dc in range(2):
-                c = lax.rem(core + dc, 2)
-                send_a(k, dp_of(x + dx, 1 - plane, c))
+                send_a(k, dp_of(x + dx, 1 - plane, lax.rem(core + dc, 2)))
+
+    def a_within(k):
+        for dx in (1, 3, 2, 0):
+            for dc in range(2):
                 if (dx, dc) != (0, 0):
-                    send_a(k, dp_of(x + dx, plane, c))
+                    send_a(k, dp_of(x + dx, plane, lax.rem(core + dc, 2)))
 
     def slot(p, j, dx, c):
         return bbuf.at[planes[p], j, lax.rem(x + dx + 4, 4) * 2 + c]
@@ -171,21 +177,21 @@
             for i, dx in enumerate((0, -1, 1, 2)):
                 arrived(slot(p, j, dx, 1 - core), s_recv.at[p, j, i])
 
-    def multiply(k, p):
-        lhs = abuf[k, planes[p]].reshape(8 * TOK, DROWS)
-        lhs_t[...] = jnp.transpose(lhs)
+    def multiply(k, p, lo=0, hi=CHUNKS):
+        depth = (hi - lo) * 8 * CROWS
+        lhs_t[:, :depth] = jnp.transpose(abuf[k, planes[p], lo:hi].reshape(depth, DROWS))
 
         def tile(t, carry):
             at = pl.ds(pl.multiple_of(t * TILE, TILE), TILE)
-            rhs = bbuf[planes[p], :, :, :, at].reshape(8 * TOK, TILE)
-            part = jnp.dot(lhs_t[...], rhs, preferred_element_type=jnp.float32)
-            if p == 0:
+            rhs = bbuf[planes[p], lo:hi, :, :, at].reshape(depth, TILE)
+            part = jnp.dot(lhs_t[:, :depth], rhs, preferred_element_type=jnp.float32)
+            if p == 0 and lo == 0:
                 grad[:, at] = part
             else:
                 grad[:, at] += part
             return carry
 
-        lax.fori_loop(0, COLS // TILE, tile, 0)
+        lax.fori_loop(0, COLS // TILE, tile, 0, unroll=True)
 
     bias_one = 1.0 - beta_one**step_count
     bias_two = 1.0 - beta_two**step_count
@@ -207,7 +213,7 @@
             value[pl.ds(r, 32), at] = w.astype(jnp.bfloat16)
             return carry
 
-        lax.fori_loop(0, (DROWS // 32) * (COLS // TILE), piece, 0)
+        lax.fori_loop(0, (DROWS // 32) * (COLS // TILE), piece, 0, unroll=4)
 
     lane_fold = lax.broadcasted_iota(jnp.int32, (FOLD, LANES), 1)
     lane_all = lax.broadcasted_iota(jnp.int32, (DROWS, LANES), 1)
@@ -270,25 +276,27 @@
     for j in range(CHUNKS):
         z_out(j)
         center(0, j)
-    all_a(0)
+    a_within(0)
     for k in range(PARTS):
         for j in range(CHUNKS):
             abuf[k, plane, j, x * 2 + core] = og[j, :, a_columns(k, dp)]
 
+    for load in loads[8:]:
+        load.wait()
     wide = lax.broadcasted_iota(jnp.int32, (GROUPS, 256), 1) // GROUPS
     high = lax.broadcasted_iota(jnp.int32, (GROUPS, 1), 0)
     have = jnp.zeros((GROUPS, 1), jnp.int32)
     wanted = jnp.zeros((GROUPS, 1), jnp.int32)
     for u in range(GROUPS):
-        have = jnp.where(high == u, lsm_ref[ex * GROUPS + u], have)
-        wanted = jnp.where(high == u, rsm_ref[ex * GROUPS + u], wanted)
+        have = jnp.where(high == u, lsm_ref[0, ex * GROUPS + u], have)
+        wanted = jnp.where(high == u, rsm_ref[0, ex * GROUPS + u], wanted)
     target = jnp.max(jnp.where(rrow[...] == have, wide, 0), axis=1, keepdims=True)
     source = jnp.max(jnp.where(lrow[...] == wanted, wide, 0), axis=1, keepdims=True)
     low = lax.broadcasted_iota(jnp.int32, (GROUPS, 128), 1)
     high = lax.broadcasted_iota(jnp.int32, (GROUPS, 128), 0)
     index_v[0:1, :] = jnp.max(jnp.where(target == low, high, 0), axis=0, keepdims=True)
     index_v[1:2, :] = jnp.max(jnp.where(high == low, source, 0), axis=0, keepdims=True)
-    to_scalar = pltpu.make_async_copy(index_v, index, load_sem.at[8])
+    to_scalar = pltpu.make_async_copy(index_v, index, load_sem.at[10])
 
     sides(0, 0)
     sides(0, 1)
@@ -297,6 +305,7 @@
     sides(0, 2)
     sides(0, 3)
     z_in(1)
+    a_across(0)
     opposite(0, 0)
     opposite(0, 1)
     z_in(2)
@@ -304,16 +313,18 @@
     opposite(0, 3)
     sides(1, 0)
     z_in(3)
-    all_a(1)
+    a_across(1)
+    a_within(1)
+    to_scalar.wait()
+    for load in loads[5:8]:
+        load.wait()
     sides(1, 1)
-    sides(1, 2)
-    sides(1, 3)
-    to_scalar.wait()
-    for load in loads[5:]:
-        load.wait()
     wait_sibling(0)
     wait_a(0, 0)
-    multiply(0, 0)
+    multiply(0, 0, 0, 2)
+    sides(1, 2)
+    multiply(0, 0, 2, 4)
+    sides(1, 3)
     for j in range(CHUNKS):
         opposite(1, j)
     wait_sibling(1)
@@ -337,7 +348,6 @@
 
 def step_call(hidden, outgrad, row_expert, counts, learner_map, rollout_map, master, mom1, mom2):
     vmem = pl.BlockSpec(memory_space=pltpu.VMEM)
-    smem = pl.BlockSpec(memory_space=pltpu.SMEM)
     hbm = pl.BlockSpec(memory_space=pltpu.HBM)
     dma = pltpu.SemaphoreType.DMA
     state = pltpu.VMEM((WIDTH, COLS), jnp.float32)
@@ -349,7 +359,7 @@
         step_kernel,
         name="grad_update_spread",
         out_shape=(state, state, state, pltpu.VMEM((WIDTH, COLS), jnp.bfloat16)),
-        in_specs=[hbm, hbm, hbm, hbm, hbm, smem, smem, smem, hbm, hbm, hbm],
+        in_specs=[hbm] * 5 + [pl.BlockSpec(memory_space=pltpu.SMEM)] + [hbm] * 3,
         out_specs=(vmem, vmem, vmem, vmem),
         scratch_shapes=[
             pltpu.VMEM((TOK, COLS), jnp.bfloat16),
@@ -357,6 +367,8 @@
             pltpu.VMEM((1, TOK), jnp.int32),
             pltpu.VMEM((1, 256), jnp.int32),
             pltpu.VMEM((1, 256), jnp.int32),
+            pltpu.SMEM((1, 256), jnp.int32),
+            pltpu.SMEM((1, 256), jnp.int32),
             pltpu.VMEM((WIDTH, COLS), jnp.float32),
             pltpu.VMEM((WIDTH, COLS), jnp.float32),
             pltpu.VMEM((WIDTH, COLS), jnp.float32),
@@ -371,7 +383,7 @@
             pltpu.VMEM((PARTS, GROUPS, PACKED, LANES), jnp.bfloat16),
             pltpu.VMEM((GROUPS, PACKED, LANES), jnp.bfloat16),
             pltpu.VMEM((GROUPS, PACKED, LANES), jnp.bfloat16),
-            dma((9,)),
+            dma((11,)),
             dma((PARTS, 16)), dma((PARTS, 16)),
             dma((CHUNKS,)), dma((CHUNKS,)),
             dma((2, CHUNKS, 2)), dma((2, CHUNKS, 2)),
@@ -389,8 +401,6 @@
         far(learner_map.reshape(1, 256)),
         far(rollout_map.reshape(1, 256)),
         counts,
-        learner_map,
-        rollout_map,
         far(master),
         far(mom1),
         far(mom2),

time: 89.9 us -> 87.9 us (0.978)
  Pallas kernels: 88.5 us -> 86.5 us
    pallas_call x1, Pallas kernels: 85.7 us -> 83.7 us  [step_call(): pl.pallas_call(step_kernel, name='grad_update_spread', out_shape=(state,...]
where the time goes in v3:
time: 87.9 us; the launch traced here: 87.8 us
  Pallas kernels  86.5 us (98%)
  between operations  1.29 us (1%)
    pallas_call x1, Pallas kernels, step_call(): pl.pallas_call(step_kernel, name='grad_update_spread', out_shape=(state,...  83.7 us
    pallas_call x1, Pallas kernels, land_call(): pl.pallas_call(land_kernel, name='land_outputs', out_shape=tuple((jax.Sha...  2.77 us

profile of v3, /device:TPU:1, one launch (start us, length us, event | category | flops | bytes accessed | tf_op | source)
XLA Modules:
  0.0 87.8 jit_solution(16035690733264588187)
XLA Ops:
  1.3 83.7 %grad_update_spread.1 = (f32[256,1792]{1,0:T(8,128)S(1)}, f32[256,1792]{1,0:T(8,128)S(1)}, f32[256,1792]{1,0:T(8,128)S(1)}, bf16[256,1792]{1,0:T(8,128)(2,1)S(1)}) custom-call(bf16[128,1792]{1,0:T(8,128)(2,1)} %bitcast.5, bf16[4,32,4096]{2,1,0:T(8,128)(2,1)} %bitcast.4, s32[1,128]{1,0:T(1,128)} %rexp_ref.1, s32[1,256]{1,0:T(1,128)} %bitcast.6, ...), custom_call_target="tpu_custom_call" | custom-call | tf_op jit(solution)/shard_map/grad_update_spread/pallas_call | solution.py:358
  85.0 2.8 %land_outputs.1 = (f32[256,1792]{1,0:T(8,128)}, f32[256,1792]{1,0:T(8,128)}, f32[256,1792]{1,0:T(8,128)}, bf16[256,1792]{1,0:T(8,128)(2,1)}) custom-call(f32[256,1792]{1,0:T(8,128)S(1)} %get-tuple-element.8.refs_0_, f32[256,1792]{1,0:T(8,128)S(1)} %get-tuple-element.9.refs_1_, f32[256,1792]{1,0:T(8,128)S(1)} %get-tuple-element.10.refs_2_, ...), custom_call_target="tpu_custom_call" | custom-call | tf_op jit(solution)/shard_map/land_outputs/pallas_call | solution.py:420

commit v4 on v3

--- a/solution.py
+++ b/solution.py
@@ -224,16 +224,11 @@
 
     def pack():
         for u in range(GROUPS):
-            block, off = divmod(u * UNIT, LANES)
-            one = shifted(value[:, block * LANES : (block + 1) * LANES], -off)
-            if off + UNIT > LANES:
-                two = shifted(value[:, (block + 1) * LANES : (block + 2) * LANES], -off)
-                one = jnp.where(lane_all < LANES - off, one, two)
-            last = one[PACKED:]
+            at = u * UNIT
+            packed[u, :, :UNIT] = value[:PACKED, at : at + UNIT]
             for g in range(PACKED // FOLD):
-                extra = shifted(last, UNIT - 16 * g)
-                mine = one[g * FOLD : (g + 1) * FOLD]
-                packed[u, g * FOLD : (g + 1) * FOLD, :] = jnp.where(lane_fold < UNIT, mine, extra)
+                extra = value[PACKED:, at + 16 * g : at + 16 * g + 16]
+                packed[u, g * FOLD : (g + 1) * FOLD, UNIT:] = extra
 
     def spread(k):
         def to_slot(i, carry):
@@ -340,10 +335,12 @@
     update(1)
     pack()
     spread(1)
+    for copy in started[: 1 - GROUPS]:
+        copy.wait_send()
     collect(0)
+    for copy in started[1 - GROUPS :]:
+        copy.wait_send()
     collect(1)
-    for copy in started:
-        copy.wait_send()
 
 
 def step_call(hidden, outgrad, row_expert, counts, learner_map, rollout_map, master, mom1, mom2):

time: 87.9 us -> 87.1 us (level)
  no operation moved by 1% of the time
where the time goes in v4:
time: 87.1 us; the launch traced here: 87 us
  Pallas kernels  85.7 us (98%)
  between operations  1.29 us (1%)
    pallas_call x1, Pallas kernels, step_call(): pl.pallas_call(step_kernel, name='grad_update_spread', out_shape=(state,...  82.9 us
    pallas_call x1, Pallas kernels, land_call(): pl.pallas_call(land_kernel, name='land_outputs', out_shape=tuple((jax.Sha...  2.77 us

profile of v4, /device:TPU:1, one launch (start us, length us, event | category | flops | bytes accessed | tf_op | source)
XLA Modules:
  0.0 87.0 jit_solution(932906312479028222)
XLA Ops:
  1.3 82.9 %grad_update_spread.1 = (f32[256,1792]{1,0:T(8,128)S(1)}, f32[256,1792]{1,0:T(8,128)S(1)}, f32[256,1792]{1,0:T(8,128)S(1)}, bf16[256,1792]{1,0:T(8,128)(2,1)S(1)}) custom-call(bf16[128,1792]{1,0:T(8,128)(2,1)} %bitcast.5, bf16[4,32,4096]{2,1,0:T(8,128)(2,1)} %bitcast.4, s32[1,128]{1,0:T(1,128)} %rexp_ref.1, s32[1,256]{1,0:T(1,128)} %bitcast.6, ...), custom_call_target="tpu_custom_call" | custom-call | tf_op jit(solution)/shard_map/grad_update_spread/pallas_call | solution.py:355
  84.2 2.8 %land_outputs.1 = (f32[256,1792]{1,0:T(8,128)}, f32[256,1792]{1,0:T(8,128)}, f32[256,1792]{1,0:T(8,128)}, bf16[256,1792]{1,0:T(8,128)(2,1)}) custom-call(f32[256,1792]{1,0:T(8,128)S(1)} %get-tuple-element.8.refs_0_, f32[256,1792]{1,0:T(8,128)S(1)} %get-tuple-element.9.refs_1_, f32[256,1792]{1,0:T(8,128)S(1)} %get-tuple-element.10.refs_2_, ...), custom_call_target="tpu_custom_call" | custom-call | tf_op jit(solution)/shard_map/land_outputs/pallas_call | solution.py:417

commit v5 on v4

--- a/solution.py
+++ b/solution.py
@@ -236,7 +236,7 @@
             return carry
 
         lax.fori_loop(0, GROUPS, to_slot, 0)
-        for i in range(1, GROUPS):
+        for i in (2, 6, 10, 14, 1, 3, 5, 7, 9, 11, 13, 15, 8, 4, 12):
             to = lax.rem(ex + i, GROUPS)
             send(sends.at[k, i], recvs[k].at[ex], e_send.at[k, i], e_recv.at[k, i], (dp, to))
         recvs[k][ex] = sends[k, 0]

time: 87.1 us -> 86.1 us (0.989)
  Pallas kernels: 85.7 us -> 84.5 us
    pallas_call x1, Pallas kernels: 82.9 us -> 81.7 us  [step_call(): pl.pallas_call(step_kernel, name='grad_update_spread', out_shape=(state,...]
where the time goes in v5:
time: 86.1 us; the launch traced here: 85.8 us
  Pallas kernels  84.5 us (98%)
  between operations  1.29 us (1%)
    pallas_call x1, Pallas kernels, step_call(): pl.pallas_call(step_kernel, name='grad_update_spread', out_shape=(state,...  81.7 us
    pallas_call x1, Pallas kernels, land_call(): pl.pallas_call(land_kernel, name='land_outputs', out_shape=tuple((jax.Sha...  2.77 us

profile of v5, /device:TPU:1, one launch (start us, length us, event | category | flops | bytes accessed | tf_op | source)
XLA Modules:
  0.0 85.8 jit_solution(3518569655937903114)
XLA Ops:
  1.3 81.7 %grad_update_spread.1 = (f32[256,1792]{1,0:T(8,128)S(1)}, f32[256,1792]{1,0:T(8,128)S(1)}, f32[256,1792]{1,0:T(8,128)S(1)}, bf16[256,1792]{1,0:T(8,128)(2,1)S(1)}) custom-call(bf16[128,1792]{1,0:T(8,128)(2,1)} %bitcast.5, bf16[4,32,4096]{2,1,0:T(8,128)(2,1)} %bitcast.4, s32[1,128]{1,0:T(1,128)} %rexp_ref.1, s32[1,256]{1,0:T(1,128)} %bitcast.6, ...), custom_call_target="tpu_custom_call" | custom-call | tf_op jit(solution)/shard_map/grad_update_spread/pallas_call | solution.py:355
  83.0 2.8 %land_outputs.1 = (f32[256,1792]{1,0:T(8,128)}, f32[256,1792]{1,0:T(8,128)}, f32[256,1792]{1,0:T(8,128)}, bf16[256,1792]{1,0:T(8,128)(2,1)}) custom-call(f32[256,1792]{1,0:T(8,128)S(1)} %get-tuple-element.8.refs_0_, f32[256,1792]{1,0:T(8,128)S(1)} %get-tuple-element.9.refs_1_, f32[256,1792]{1,0:T(8,128)S(1)} %get-tuple-element.10.refs_2_, ...), custom_call_target="tpu_custom_call" | custom-call | tf_op jit(solution)/shard_map/land_outputs/pallas_call | solution.py:417

commit v6 on v5

--- a/solution.py
+++ b/solution.py
@@ -213,7 +213,7 @@
             value[pl.ds(r, 32), at] = w.astype(jnp.bfloat16)
             return carry
 
-        lax.fori_loop(0, (DROWS // 32) * (COLS // TILE), piece, 0, unroll=4)
+        lax.fori_loop(0, (DROWS // 32) * (COLS // TILE), piece, 0, unroll=7)
 
     lane_fold = lax.broadcasted_iota(jnp.int32, (FOLD, LANES), 1)
     lane_all = lax.broadcasted_iota(jnp.int32, (DROWS, LANES), 1)

time: 86.1 us -> 86.1 us (level)
  no operation moved by 1% of the time
where the time goes in v6:
time: 86.1 us; the launch traced here: 85.7 us
  Pallas kernels  84.5 us (98%)
  between operations  1.29 us (1%)
    pallas_call x1, Pallas kernels, step_call(): pl.pallas_call(step_kernel, name='grad_update_spread', out_shape=(state,...  81.7 us
    pallas_call x1, Pallas kernels, land_call(): pl.pallas_call(land_kernel, name='land_outputs', out_shape=tuple((jax.Sha...  2.77 us

profile of v6, /device:TPU:1, one launch (start us, length us, event | category | flops | bytes accessed | tf_op | source)
XLA Modules:
  0.0 85.7 jit_solution(7748135234078918693)
XLA Ops:
  1.3 81.7 %grad_update_spread.1 = (f32[256,1792]{1,0:T(8,128)S(1)}, f32[256,1792]{1,0:T(8,128)S(1)}, f32[256,1792]{1,0:T(8,128)S(1)}, bf16[256,1792]{1,0:T(8,128)(2,1)S(1)}) custom-call(bf16[128,1792]{1,0:T(8,128)(2,1)} %bitcast.5, bf16[4,32,4096]{2,1,0:T(8,128)(2,1)} %bitcast.4, s32[1,128]{1,0:T(1,128)} %rexp_ref.1, s32[1,256]{1,0:T(1,128)} %bitcast.6, ...), custom_call_target="tpu_custom_call" | custom-call | tf_op jit(solution)/shard_map/grad_update_spread/pallas_call | solution.py:355
  83.0 2.8 %land_outputs.1 = (f32[256,1792]{1,0:T(8,128)}, f32[256,1792]{1,0:T(8,128)}, f32[256,1792]{1,0:T(8,128)}, bf16[256,1792]{1,0:T(8,128)(2,1)}) custom-call(f32[256,1792]{1,0:T(8,128)S(1)} %get-tuple-element.8.refs_0_, f32[256,1792]{1,0:T(8,128)S(1)} %get-tuple-element.9.refs_1_, f32[256,1792]{1,0:T(8,128)S(1)} %get-tuple-element.10.refs_2_, ...), custom_call_target="tpu_custom_call" | custom-call | tf_op jit(solution)/shard_map/land_outputs/pallas_call | solution.py:417
